TPU v7x, 32 devices: a whole 2x2x4 slice. The times are simulated.
32 devices in a mesh: dp: 8 (over z, y), mp: 4 (over x, core).
Axes of the slice: x: 2, y: 2, z: 4, core: 2. Of those that a mesh axis runs over, the one named last changes fastest.
Arguments:
- logits: bfloat16 [1024, 16384], P('dp', 'mp'), may hold values from -72 to 240
- targets: int32 [1024], P('dp'), may hold values from 0 to 16383
- resp_mask: int32 [1024], P('dp'), may hold values from 0 to 1, as said below
- rewards: int32 [8], P('dp'), may hold values from 0 to 10
- groups: int32 [8], P('dp'), may hold values from 0 to 1, as said below
- unit_grad: bfloat16 [1024, 8192], P(('dp', 'mp')), may hold values from -192 to 192
- mix: bfloat16 [1024, 2048], P('dp', 'mp'), may hold values from -6 to 6
- w_out: bfloat16 [2048, 8192], P('mp', 'dp'), may hold values from -0.125 to 0.125
Outputs:
- token_logprob: float32 [1024], P('dp')
- policy_loss: float32 [], replicated
- grad_mix: bfloat16 [1024, 2048], P('dp', 'mp')
- grad_w_out: bfloat16 [2048, 8192], P('mp', 'dp')
Inputs may be any that keep to these rules, and one draw needn't show every extreme that they name: `resp_mask`: in each sample the response mask is a run of ones followed by zeros, with at least 32 ones. `groups`: each prompt id names exactly 4 samples.
All inputs are finite; a program needn't handle non-finite values.
Results may differ from a plain program's by a relative error of at most 0.005.
Values may be sent and summed in bfloat16 or wider, within the bound.
A program may use at most 64 MiB of HBM per device.

v0:
```python
import jax
import jax.numpy as jnp
from jax import lax
from jax.sharding import PartitionSpec as P

K = 4


def shards(logits, targets, resp_mask, rewards, groups, unit_grad, mix, w_out):
    tok_rows, vocab_dev = logits.shape
    mp_lane = lax.axis_index("mp")
    local_target = targets - mp_lane * vocab_dev
    present = (local_target >= 0) & (local_target < vocab_dev)
    picked = jnp.take_along_axis(logits, jnp.clip(local_target, 0, vocab_dev - 1)[:, None], axis=1)[
        :, 0
    ]
    picked = jnp.where(present, picked.astype(jnp.float32), 0.0)
    local_max = jnp.max(logits, axis=1).astype(jnp.float32)
    highest = lax.pmax(local_max, "mp")
    local_sum = jnp.sum(jnp.exp(logits.astype(jnp.float32) - highest[:, None]), axis=1)
    summed, target_logit = lax.psum((local_sum, picked), "mp")
    logprob = target_logit - (highest + jnp.log(summed))
    mask_float = resp_mask.astype(jnp.float32)
    local_count = jnp.sum(mask_float)
    reward_float = rewards.astype(jnp.float32)
    prompt_slots = jnp.arange(lax.axis_size("dp") // K, dtype=jnp.int32)
    own_slot = (prompt_slots == groups[0]).astype(jnp.float32)
    group_total, token_count = lax.psum((own_slot * reward_float[0], local_count), "dp")
    own_total = jnp.sum(own_slot * group_total)
    advantage = reward_float[0] - (own_total - reward_float[0]) / (K - 1)
    weight = advantage * mask_float / token_count
    policy_loss = lax.psum(-jnp.sum(weight * logprob), "dp")
    sub_rows = unit_grad.shape[0]
    part_weight = lax.dynamic_slice_in_dim(weight, mp_lane * sub_rows, sub_rows)
    grad_local = (-part_weight[:, None] * unit_grad.astype(jnp.float32)).astype(jnp.bfloat16)
    grad_group = lax.all_gather(grad_local, "mp", axis=0, tiled=True)
    grad_mix = lax.dot_general(
        grad_group,
        lax.all_gather(w_out, "dp", axis=1, tiled=True),
        (((1,), (1,)), ((), ())),
        preferred_element_type=jnp.float32,
    ).astype(jnp.bfloat16)
    grad_every = lax.all_to_all(grad_group, "dp", split_axis=1, concat_axis=0, tiled=True)
    grad_w_out = lax.dot_general(
        lax.all_gather(mix, "dp", axis=0, tiled=True),
        grad_every,
        (((0,), (0,)), ((), ())),
        preferred_element_type=jnp.float32,
    ).astype(jnp.bfloat16)
    return (logprob, policy_loss, grad_mix, grad_w_out)


def solution(mesh):
    return jax.shard_map(
        shards,
        mesh=mesh,
        in_specs=(
            P("dp", "mp"),
            P("dp"),
            P("dp"),
            P("dp"),
            P("dp"),
            P(("dp", "mp"), None),
            P("dp", "mp"),
            P("mp", "dp"),
        ),
        out_specs=(P("dp"), P(), P("dp", "mp"), P("mp", "dp")),
        check_vma=False,
    )
```

profile of v0, /device:TPU:0, one launch (start us, length us, event | category | flops | bytes accessed | tf_op | source)
XLA Modules:
  0.0 279.9 jit_solution(4905215738061434298)
XLA Ops:
  7.2 1.3 convert_reduce_fusion
  9.9 23.8 %all-reduce = (f32[]{:T(128)}, f32[2]{0:T(128)S(1)}) all-reduce(f32[]{:T(128)} %convert_reduce_fusion, f32[2]{0:T(128)S(1)} %compare_select_fusion.2), channel_id=1, replica_groups=mesh['dp'=8,'mp'=4] {'dp'}, use_global_device_ids=true, to_apply=%region_8.9 | all-reduce | flops 3 | bytes 24 | tf_op jit(solution)/shard_map/psum | solution.py:28
  33.6 0.6 fusion.1
  34.9 0.7 fusion.2
  35.6 2.3 gather_fusion
  37.9 0.7 and_select_fusion.1
  38.5 1.4 reduce_max.9
  40.0 5.7 %pmax.7 = f32[128]{0:T(128)S(1)} all-reduce(bf16[128]{0:T(256)(128)(2,1)S(1)} %reduce_max.9), channel_id=1, replica_groups=mesh['dp'=8,'mp'=4] {'mp'}, use_global_device_ids=true, to_apply=%region_2.3 | all-reduce | flops 128 | bytes 768 | tf_op jit(solution)/shard_map/pmax | solution.py:19
  45.6 1.7 exponential_reduce_fusion
  47.4 6.6 %all-reduce.1 = (f32[128]{0:T(128)S(1)}, f32[128]{0:T(128)S(1)}) all-reduce(f32[128]{0:T(128)S(1)} %and_select_fusion.1, f32[128]{0:T(128)S(1)} %exponential_reduce_fusion), channel_id=1, replica_groups=mesh['dp'=8,'mp'=4] {'mp'}, use_global_device_ids=true, to_apply=%region_0.1 | all-reduce | flops 256 | bytes 2048 | tf_op jit(solution)/shard_map/psum | solution.py:21
  53.9 1.8 multiply_reduce_fusion
  55.8 0.9 multiply_convert_fusion
  56.8 0.7 all-gather.8.cloned.1.call-update
  57.5 0.7 all-gather.6.cloned.1.call-update
  58.2 18.0 %all-gather.4.cloned.1.call-done = bf16[128,8192]{1,0:T(8,128)(2,1)} async-done(((bf16[32,8192]{1,0:T(8,128)(2,1)}), bf16[128,8192]{1,0:T(8,128)(2,1)}) %all-gather.4.cloned.1.call-update) | async-done | bytes 2097168 | tf_op jit(solution)/shard_map/all_gather | solution.py:36
  76.2 4.1 %copy.17 = bf16[128,8192]{0,1:T(8,128)(2,1)} copy(bf16[128,8192]{1,0:T(8,128)(2,1)} %all-gather.4.cloned.1.call-done) | data formatting | bytes 4194304 | tf_op jit(solution)/shard_map/all_gather | solution.py:36
  80.3 5.5 %all-to-all-start = ((bf16[128,8,1024]{0,2,1:T(8,128)(2,1)}), bf16[128,8,1024]{0,2,1:T(8,128)(2,1)S(1)}, u32[]{:S(2)}, u32[]{:S(2)}) async-start(bf16[128,8,1024]{0,2,1:T(8,128)(2,1)} %bitcast.20), calls=%async_computation | async-start | bytes 4194304 | tf_op jit(solution)/shard_map/all_to_all | solution.py:43
  86.4 56.0 %psum.39 = f32[]{:T(128)} all-reduce(f32[]{:T(128)S(6)} %neg.7), channel_id=1, replica_groups=mesh['dp'=8,'mp'=4] {'dp'}, use_global_device_ids=true, to_apply=%region_10.11 | all-reduce | flops 1 | bytes 8 | tf_op jit(solution)/shard_map/psum | solution.py:32
  142.5 4.6 %all-to-all-done = bf16[128,8,1024]{0,2,1:T(8,128)(2,1)S(1)} async-done(((bf16[128,8,1024]{0,2,1:T(8,128)(2,1)}), bf16[128,8,1024]{0,2,1:T(8,128)(2,1)S(1)}, u32[]{:S(2)}, u32[]{:S(2)}) %all-to-all-start) | async-done | bytes 2097184 | tf_op jit(solution)/shard_map/all_to_all | solution.py:43
  147.1 2.6 copy.18
  149.7 3.4 %fusion = bf16[512,1024]{0,1:T(8,128)(2,1)S(1)} fusion(bf16[1024,1024]{1,0:T(8,128)(2,1)} %bitcast.21, bf16[1024,512]{1,0:T(8,128)(2,1)} %all-gather.8.cloned.1.call-done), kind=kOutput, calls=%fused_computation.3 | convolution fusion | flops 1074266112 | bytes 4194304 | tf_op jit(solution)/shard_map/dot_general | solution.py:44
  153.1 1.3 copy.19
  154.4 112.0 %all-gather.6.cloned.1.call-done = bf16[512,8192]{1,0:T(8,128)(2,1)} async-done(((bf16[512,1024]{1,0:T(8,128)(2,1)}), bf16[512,8192]{1,0:T(8,128)(2,1)}) %all-gather.6.cloned.1.call-update) | async-done | bytes 8388624 | tf_op jit(solution)/shard_map/all_gather | solution.py:39
  266.4 7.0 %convolution_convert_fusion.1 = bf16[128,512]{1,0:T(8,128)(2,1)} fusion(bf16[128,8192]{1,0:T(8,128)(2,1)S(1)} %copy-done, bf16[512,8192]{1,0:T(8,128)(2,1)} %all-gather.6.cloned.1.call-done), kind=kOutput, calls=%fused_computation.4 | convolution fusion | flops 1073807360 | bytes 10616832 | tf_op jit(solution)/shard_map/dot_general | solution.py:37
  (16 shorter events, 0.3 us)
Async XLA Ops:
  7.2 46.8 %copy-start.2 = (s32[128]{0:T(128)S(1)}, s32[128]{0:T(128)}, u32[]{:S(2)}) copy-start(s32[128]{0:T(128)} %param.10) | copy-start | bytes 1540
  7.2 48.6 %copy-start.1 = (bf16[32,8192]{1,0:T(8,128)(2,1)S(1)}, bf16[32,8192]{1,0:T(8,128)(2,1)}, u32[]{:S(2)}) copy-start(bf16[32,8192]{1,0:T(8,128)(2,1)} %param.13) | copy-start | bytes 1572868
  7.2 69.0 %all-gather.4.cloned.1.call-start = ((), (), s32[]{:S(2)}) async-start(), calls=%async_computation.1 | async-start | bytes 2621440 | tf_op jit(solution)/shard_map/all_gather | solution.py:36
  56.7 92.9 %all-gather.8.cloned.1.call-start = ((), (), s32[]{:S(2)}) async-start(), calls=%async_computation.3 | async-start | bytes 1179648 | tf_op jit(solution)/shard_map/all_gather | solution.py:45
  57.5 208.9 %all-gather.6.cloned.1.call-start = ((), (), s32[]{:S(2)}) async-start(), calls=%async_computation.2 | async-start | bytes 9437184 | tf_op jit(solution)/shard_map/all_gather | solution.py:39
  80.3 66.8 %all-to-all-start = ((bf16[128,8,1024]{0,2,1:T(8,128)(2,1)}), bf16[128,8,1024]{0,2,1:T(8,128)(2,1)S(1)}, u32[]{:S(2)}, u32[]{:S(2)}) async-start(bf16[128,8,1024]{0,2,1:T(8,128)(2,1)} %bitcast.20), calls=%async_computation | async-start | bytes 4194304 | tf_op jit(solution)/shard_map/all_to_all | solution.py:43
  153.1 113.3 %copy-start = (bf16[128,8192]{1,0:T(8,128)(2,1)S(1)}, bf16[128,8192]{1,0:T(8,128)(2,1)}, u32[]{:S(2)}) copy-start(bf16[128,8192]{1,0:T(8,128)(2,1)} %all-gather.4.cloned.1.call-done) | copy-start | bytes 6291460
Sparse Core Ops, SparseCore 0:
  56.9 19.2 all-gather.3
  78.3 63.1 all-gather.7
  143.7 122.6 all-gather.5
where the time goes:
time: 280 us
  waiting for transfers between devices  136 us (49%)
  blocking collectives  92 us (33%)
  between operations  16.4 us (6%)
  matrix products  10.4 us (4%)
  local copies, waits for them, and re-layouts  10.3 us (4%)
  other arithmetic  9.22 us (3%)
  starting transfers between devices  5.63 us (2%)
    all_gather x1, waiting for transfers between devices, shards(): lax.all_gather(w_out, 'dp', axis=1, tiled=True)  112 us
    psum x1, blocking collectives, shards(): policy_loss = lax.psum(-jnp.sum(weight * logprob), 'dp')  56 us
    psum x1, blocking collectives, shards(): lax.psum((own_slot * reward_float[0], local_count), 'dp')  23.8 us
    all_gather x1, waiting for transfers between devices, shards(): grad_group = lax.all_gather(grad_local, 'mp', axis=0, tiled=True)  18 us
    dot_general x1, matrix products, shards(): lax.dot_general(grad_group, lax.all_gather(w_out, 'dp', axis=1, tiled=Tru...  6.96 us
    psum x1, blocking collectives, shards(): summed, target_logit = lax.psum((local_sum, picked), 'mp')  6.56 us
    pmax x1, blocking collectives, shards(): highest = lax.pmax(local_max, 'mp')  5.66 us
  transfers between devices with their start and end apart: 4, of which 3 were waited for; matrix products, arithmetic and copies ran while one was open for 4% of the time, Pallas kernels for 0%

commit v1 on v0

--- a/solution.py
+++ b/solution.py
@@ -4,6 +4,13 @@
 from jax.sharding import PartitionSpec as P
 
 K = 4
+
+
+def exchange_gather(array, mesh_axis, dim):
+    devices = lax.axis_size(mesh_axis)
+    blocks = jnp.stack([array for _ in range(devices)])
+    blocks = lax.all_to_all(blocks, mesh_axis, split_axis=0, concat_axis=0)
+    return jnp.concatenate(blocks, axis=dim)
 
 
 def shards(logits, targets, resp_mask, rewards, groups, unit_grad, mix, w_out):
@@ -33,7 +40,7 @@
     sub_rows = unit_grad.shape[0]
     part_weight = lax.dynamic_slice_in_dim(weight, mp_lane * sub_rows, sub_rows)
     grad_local = (-part_weight[:, None] * unit_grad.astype(jnp.float32)).astype(jnp.bfloat16)
-    grad_group = lax.all_gather(grad_local, "mp", axis=0, tiled=True)
+    grad_group = exchange_gather(grad_local, "mp", 0)
     grad_mix = lax.dot_general(
         grad_group,
         lax.all_gather(w_out, "dp", axis=1, tiled=True),

time: 280 us -> 228 us (0.81)
  waiting for transfers between devices: 136 us -> 49.3 us
  blocking collectives: 92 us -> 134 us
  other arithmetic: 9.22 us -> 5.28 us
    all_gather x1, waiting for transfers between devices: 112 us -> 30.5 us  [shards(): lax.all_gather(w_out, 'dp', axis=1, tiled=True)]
    all_to_all x0 -> x1, blocking collectives: none -> 28.1 us  [exchange_gather(): blocks = lax.all_to_all(blocks, mesh_axis, split_axis=0, concat_axis=0)]
    all_gather x1 -> x0, waiting for transfers between devices: 18 us -> none  [shards(): grad_group = lax.all_gather(grad_local, 'mp', axis=0, tiled=True)]
    psum x1, blocking collectives: 56 us -> 69.7 us  [shards(): policy_loss = lax.psum(-jnp.sum(weight * logprob), 'dp')]
    all_to_all x1, waiting for transfers between devices: 4.61 us -> 17.5 us  [shards(): lax.all_to_all(grad_group, 'dp', split_axis=1, concat_axis=0, tiled=True)]
    all_gather x1 -> x0, local copies, waits for them, and re-layouts: 4.07 us -> none  [shards(): grad_group = lax.all_gather(grad_local, 'mp', axis=0, tiled=True)]
  transfers between devices with their start and end apart: 4 -> 3, of which waited for: 3 -> 2; matrix products, arithmetic and copies ran while one was open for 4% -> 7% of each run, Pallas kernels for 0% -> 0%
where the time goes in v1:
time: 228 us
  blocking collectives  134 us (59%)
  waiting for transfers between devices  49.3 us (22%)
  between operations  16.7 us (7%)
  matrix products  10.1 us (4%)
  local copies, waits for them, and re-layouts  7.66 us (3%)
  other arithmetic  5.28 us (2%)
  starting transfers between devices  4.43 us (2%)
    psum x1, blocking collectives, shards(): policy_loss = lax.psum(-jnp.sum(weight * logprob), 'dp')  69.7 us
    all_gather x1, waiting for transfers between devices, shards(): lax.all_gather(w_out, 'dp', axis=1, tiled=True)  30.5 us
    all_to_all x1, blocking collectives, exchange_gather(): blocks = lax.all_to_all(blocks, mesh_axis, split_axis=0, concat_axis=0)  28.1 us
    psum x1, blocking collectives, shards(): lax.psum((own_slot * reward_float[0], local_count), 'dp')  23.8 us
    all_to_all x1, waiting for transfers between devices, shards(): lax.all_to_all(grad_group, 'dp', split_axis=1, concat_axis=0, tiled=True)  17.5 us
    dot_general x1, matrix products, shards(): lax.dot_general(grad_group, lax.all_gather(w_out, 'dp', axis=1, tiled=Tru...  6.96 us
    psum x1, blocking collectives, shards(): summed, target_logit = lax.psum((local_sum, picked), 'mp')  6.57 us
    pmax x1, blocking collectives, shards(): highest = lax.pmax(local_max, 'mp')  6.07 us
  transfers between devices with their start and end apart: 3, of which 2 were waited for; matrix products, arithmetic and copies ran while one was open for 7% of the time, Pallas kernels for 0%

profile of v1, /device:TPU:0, one launch (start us, length us, event | category | flops | bytes accessed | tf_op | source)
XLA Modules:
  0.0 227.8 jit_solution(18152395308843807440)
XLA Ops:
  7.3 0.7 all-gather.5.cloned.1.call-update
  8.0 0.7 all-gather.3.cloned.1.call-update
  10.0 1.3 convert_reduce_fusion
  11.3 23.8 %all-reduce = (f32[]{:T(128)}, f32[2]{0:T(128)S(1)}) all-reduce(f32[]{:T(128)} %convert_reduce_fusion, f32[2]{0:T(128)S(1)} %compare_select_fusion.2), channel_id=1, replica_groups=mesh['dp'=8,'mp'=4] {'dp'}, use_global_device_ids=true, to_apply=%region_8.9 | all-reduce | flops 3 | bytes 24 | tf_op jit(solution)/shard_map/psum | solution.py:35
  35.1 0.6 fusion.1
  36.3 0.7 fusion.2
  37.0 2.3 gather_fusion
  39.3 0.2 reduce_max.9
  39.5 6.1 %pmax.7 = f32[128]{0:T(128)S(1)} all-reduce(bf16[128]{0:T(256)(128)(2,1)S(1)} %reduce_max.9), channel_id=1, replica_groups=mesh['dp'=8,'mp'=4] {'mp'}, use_global_device_ids=true, to_apply=%region_2.3 | all-reduce | flops 128 | bytes 768 | tf_op jit(solution)/shard_map/pmax | solution.py:26
  45.6 0.5 exponential_reduce_fusion
  46.1 6.6 %all-reduce.1 = (f32[128]{0:T(128)S(1)}, f32[128]{0:T(128)S(1)}) all-reduce(f32[128]{0:T(128)S(1)} %and_select_fusion.1, f32[128]{0:T(128)S(1)} %exponential_reduce_fusion), channel_id=1, replica_groups=mesh['dp'=8,'mp'=4] {'mp'}, use_global_device_ids=true, to_apply=%region_0.1 | all-reduce | flops 256 | bytes 2048 | tf_op jit(solution)/shard_map/psum | solution.py:28
  52.7 1.8 multiply_reduce_fusion
  54.5 0.2 multiply_convert_fusion
  54.7 0.2 stack.2
  54.9 28.1 %all_to_all.24 = bf16[4,32,8192]{2,1,0:T(8,128)(2,1)S(1)} all-to-all(bf16[4,32,8192]{2,1,0:T(8,128)(2,1)S(1)} %stack.2), channel_id=1, replica_groups=mesh['dp'=8,'mp'=4] {'mp'}, dimensions={0} | all-to-all | bytes 4194304 | tf_op jit(solution)/shard_map/all_to_all | solution.py:12
  83.0 1.4 copy.18
  84.4 2.4 %copy.16 = bf16[128,8,1024]{2,0,1:T(8,128)(2,1)} copy(bf16[128,8,1024]{2,1,0:T(8,128)(2,1)S(1)} %bitcast.25) | data formatting | bytes 4194304 | tf_op jit(solution)/shard_map/all_to_all | solution.py:50
  86.9 4.4 %all-to-all-start.1 = ((bf16[128,8,1024]{2,0,1:T(8,128)(2,1)}), bf16[128,8,1024]{2,0,1:T(8,128)(2,1)}, u32[]{:S(2)}, u32[]{:S(2)}) async-start(bf16[128,8,1024]{2,0,1:T(8,128)(2,1)} %copy.16), calls=%async_computation.1 | async-start | bytes 4194304 | tf_op jit(solution)/shard_map/all_to_all | solution.py:50
  91.9 69.7 %psum.39 = f32[]{:T(128)} all-reduce(f32[]{:T(128)S(6)} %neg.7), channel_id=1, replica_groups=mesh['dp'=8,'mp'=4] {'dp'}, use_global_device_ids=true, to_apply=%region_10.11 | all-reduce | flops 1 | bytes 8 | tf_op jit(solution)/shard_map/psum | solution.py:39
  161.6 17.5 %all-to-all-done.1 = bf16[128,8,1024]{2,0,1:T(8,128)(2,1)} async-done(((bf16[128,8,1024]{2,0,1:T(8,128)(2,1)}), bf16[128,8,1024]{2,0,1:T(8,128)(2,1)}, u32[]{:S(2)}, u32[]{:S(2)}) %all-to-all-start.1) | async-done | bytes 2097184 | tf_op jit(solution)/shard_map/all_to_all | solution.py:50
  179.1 3.1 %fusion = bf16[512,1024]{0,1:T(8,128)(2,1)S(1)} fusion(bf16[1024,1024]{1,0:T(8,128)(2,1)} %bitcast.7, bf16[1024,512]{1,0:T(8,128)(2,1)} %all-gather.5.cloned.1.call-done), kind=kOutput, calls=%fused_computation.3 | convolution fusion | flops 1074266112 | bytes 4194304 | tf_op jit(solution)/shard_map/dot_general | solution.py:51
  182.2 1.3 copy.17
  183.5 30.5 %all-gather.3.cloned.1.call-done = bf16[512,8192]{1,0:T(8,128)(2,1)} async-done(((bf16[512,1024]{1,0:T(8,128)(2,1)}), bf16[512,8192]{1,0:T(8,128)(2,1)}) %all-gather.3.cloned.1.call-update) | async-done | bytes 8388624 | tf_op jit(solution)/shard_map/all_gather | solution.py:46
  214.0 7.0 %convolution_convert_fusion.1 = bf16[128,512]{1,0:T(8,128)(2,1)} fusion(bf16[128,8192]{1,0:T(8,128)(2,1)S(1)} %bitcast.24, bf16[512,8192]{1,0:T(8,128)(2,1)} %all-gather.3.cloned.1.call-done), kind=kOutput, calls=%fused_computation.4 | convolution fusion | flops 1073807360 | bytes 10616832 | tf_op jit(solution)/shard_map/dot_general | solution.py:44
  (17 shorter events, 0.2 us)
Async XLA Ops:
  7.2 45.5 %copy-start.2 = (s32[128]{0:T(128)S(1)}, s32[128]{0:T(128)}, u32[]{:S(2)}) copy-start(s32[128]{0:T(128)} %param.10) | copy-start | bytes 1540
  7.2 38.9 %copy-start.3 = (s32[128]{0:T(128)S(1)}, s32[128]{0:T(128)}, u32[]{:S(2)}) copy-start(s32[128]{0:T(128)} %param.9) | copy-start | bytes 1540
  7.2 32.1 %copy-start = (bf16[128,4096]{1,0:T(8,128)(2,1)S(1)}, bf16[128,4096]{1,0:T(8,128)(2,1)}, u32[]{:S(2)}) copy-start(bf16[128,4096]{1,0:T(8,128)(2,1)} %param.8) | copy-start | bytes 3145732
  7.2 47.3 %copy-start.1 = (bf16[32,8192]{1,0:T(8,128)(2,1)S(1)}, bf16[32,8192]{1,0:T(8,128)(2,1)}, u32[]{:S(2)}) copy-start(bf16[32,8192]{1,0:T(8,128)(2,1)} %param.13) | copy-start | bytes 1572868
  7.2 154.4 %all-gather.5.cloned.1.call-start = ((), (), s32[]{:S(2)}) async-start(), calls=%async_computation.3 | async-start | bytes 1179648 | tf_op jit(solution)/shard_map/all_gather | solution.py:52
  7.9 206.1 %all-gather.3.cloned.1.call-start = ((), (), s32[]{:S(2)}) async-start(), calls=%async_computation.2 | async-start | bytes 9437184 | tf_op jit(solution)/shard_map/all_gather | solution.py:46
  86.9 92.2 %all-to-all-start.1 = ((bf16[128,8,1024]{2,0,1:T(8,128)(2,1)}), bf16[128,8,1024]{2,0,1:T(8,128)(2,1)}, u32[]{:S(2)}, u32[]{:S(2)}) async-start(bf16[128,8,1024]{2,0,1:T(8,128)(2,1)} %copy.16), calls=%async_computation.1 | async-start | bytes 4194304 | tf_op jit(solution)/shard_map/all_to_all | solution.py:50
Sparse Core Ops, SparseCore 0:
  10.1 43.0 all-gather.4
  55.4 158.5 all-gather.2
